TPU v7x, 32 devices: a whole 2x2x4 slice. The times are simulated.
32 devices in a mesh: scene: 2 (over y), pulse: 8 (over z, x), scat: 2 (over core).
Axes of the slice: x: 2, y: 2, z: 4, core: 2. Of those that a mesh axis runs over, the one named last changes fastest.
Arguments:
- positions: float32 [32768], P(('scene', 'scat')), parts along dimension 0, may hold values from -1000 to 1000
- amplitude: float32 [2, 32768], P(None, ('scene', 'scat')), parts along dimension 1, may hold values from -3 to 3
- range_cells: int32 [32768], P(('scene', 'scat')), parts along dimension 0, may hold values from 0 to 1007
- bounce: int32 [32768], P(('scene', 'scat')), parts along dimension 0, may hold values 0 or 1
- stolt_block: int32 [512, 32], P(('pulse', 'scat')), may hold values from 0 to 30
- kernel_choice: int32 [512, 32], P(('pulse', 'scat')), may hold values from 0 to 15
- kernel_bank: float32 [16, 256, 128], replicated, may hold values from -0.375 to 0.375
Outputs:
- image: float32 [2, 1024, 4096], P(None, 'scene', ('pulse', 'scat')), parts along dimension 1
There are 2 independent parts, one for each index of `scene`. A program takes and returns all parts, laid end to end along the dimension named above; an argument that names none is the same for every part. Nothing has to cross between parts.
All inputs are finite; a program needn't handle non-finite values. No bound on the sum of `bounce` on one device may be relied on, other than what follows from the above.
Results may differ from a plain program's by a relative error of at most 0.0003.
Values sent between devices are 32-bit elements; how exact they have to be, the bound alone decides.
A program may use at most 64 MiB of HBM per device.

v0:
```python
import functools

import jax
import jax.numpy as jnp
import numpy as np
from jax import lax
from jax.experimental import pallas as pl
from jax.experimental.pallas import tpu as pltpu
from jax.sharding import PartitionSpec as P

P_SIZE = 512
F_LEN = 4096
B = 1024
SHIFT = 16
STOLT = 128
BLOCKS = 32
SPACING = 2.0
NEAR = 700000.0
BIN_SIDE = 32
GROUP = 4
CHUNK = 1024
SLOTS = 192
WIDE = 128
AHEAD = 1024
HIGH = lax.Precision.HIGH
MESH = pl.DeviceIdType.MESH
IN_HBM = pl.BlockSpec(memory_space=pltpu.HBM)
IN_VMEM = pl.BlockSpec(memory_space=pltpu.VMEM)
f32 = jnp.float32
bf16 = jnp.bfloat16


def trig_coefs():
    x = np.cos(np.pi * (np.arange(400) + 0.5) / 400) * 0.5
    u = x * x
    s = np.polynomial.chebyshev.Chebyshev.fit(u, np.sin(np.pi * x) / x, 5).convert(
        kind=np.polynomial.Polynomial
    )
    c = np.polynomial.chebyshev.Chebyshev.fit(u, np.cos(np.pi * x), 5).convert(
        kind=np.polynomial.Polynomial
    )
    return [float(v) for v in s.coef], [float(v) for v in c.coef]


def horner(u, coefs):
    acc = jnp.full_like(u, coefs[-1])
    for c in coefs[-2::-1]:
        acc = acc * u + c
    return acc


def split(x):
    hi = x.astype(bf16)
    lo = (x - hi.astype(f32)).astype(bf16)
    return hi, lo


def np_split(x):
    x = np.asarray(x, np.float64)
    hi = np.asarray(x, jnp.bfloat16)
    lo = np.asarray(x - hi.astype(np.float64), jnp.bfloat16)
    return np.stack([hi, lo])


def dots(a, b, dims):
    d = functools.partial(
        lax.dot_general, dimension_numbers=(dims, ((), ())), preferred_element_type=f32
    )
    return d(a[0], b[0]) + (d(a[0], b[1]) + d(a[1], b[0]))


def in_hbm(arrays):
    return [pltpu.with_memory_space_constraint(a, pltpu.HBM) for a in arrays]


def joined(hi, lo, axis):
    return jnp.concatenate([hi, hi, lo], axis)


def triple(x, axis):
    hi, lo = split(x)
    return jnp.concatenate([hi, lo, hi], axis)


def product(a, b, dims=((1,), (0,))):
    return lax.dot_general(a, b, (dims, ((), ())), preferred_element_type=f32)


def bin_kernel(pulse_base, pos, amp, tgt, bnc, out, acc, *, pulses, sin_c, cos_c):
    step = pl.program_id(0)
    width = pos.shape[1]

    @pl.when(step == 0)
    def _():
        acc[...] = jnp.zeros_like(acc)

    base = pulse_base[0]
    ids = base + lax.broadcasted_iota(jnp.int32, (pulses, width), 0)
    along = (ids.astype(f32) - P_SIZE // 2) * SPACING
    target = tgt[...] + SHIFT * bnc[...]
    slant = NEAR + target.astype(f32)
    offset = along - pos[...]
    square = offset * offset
    excess = square / (jnp.sqrt(slant * slant + square) + slant)
    halves = excess * -128.0
    whole = jnp.round(halves)
    r = halves - whole
    u = r * r
    odd = whole - 2.0 * jnp.floor(whole * 0.5)
    sign = 1.0 - 2.0 * odd
    sin_p = sign * r * horner(u, sin_c)
    cos_p = sign * horner(u, cos_c)
    flip = 1.0 - 2.0 * bnc[...].astype(f32)
    are = flip * amp[0:1]
    aim = flip * amp[1:2]
    re = are * cos_p - aim * sin_p
    im = are * sin_p + aim * cos_p
    steer = jnp.concatenate([re, im], 0)
    hi, lo = split(steer)
    rhs = jnp.concatenate([hi, lo], 0)
    bins = lax.broadcasted_iota(jnp.int32, (B, width), 0)
    hot = jnp.where(bins == target, 1.0, 0.0).astype(bf16)
    acc[...] += lax.dot_general(
        hot, rhs, (((1,), (1,)), ((), ())), preferred_element_type=f32
    )

    @pl.when(step == pl.num_programs(0) - 1)
    def _():
        out[...] = acc[:, : 2 * pulses] + acc[:, 2 * pulses :]


def binning(positions, amplitude, cells, bounce, pulse_base, pulses):
    count = positions.shape[0]
    width = min(2048, count)
    sin_c, cos_c = trig_coefs()
    row = lambda n: pl.BlockSpec((n, width), lambda i: (0, i))
    return pl.pallas_call(
        functools.partial(bin_kernel, pulses=pulses, sin_c=sin_c, cos_c=cos_c),
        grid=(count // width,),
        in_specs=[pl.BlockSpec(memory_space=pltpu.SMEM), row(1), row(2), row(1), row(1)],
        out_specs=pl.BlockSpec((B, 2 * pulses), lambda i: (0, 0)),
        out_shape=jax.ShapeDtypeStruct((B, 2 * pulses), f32),
        scratch_shapes=[pltpu.VMEM((B, 4 * pulses), f32)],
        name="binning",
    )(
        pulse_base.reshape(1),
        positions.reshape(1, count),
        amplitude,
        cells.reshape(1, count),
        bounce.reshape(1, count),
    )


def range_trig_coefs(degree):
    x = np.cos(np.pi * (np.arange(400) + 0.5) / 400) * 0.5
    u = x * x
    fit = lambda y: np.polynomial.chebyshev.Chebyshev.fit(u, y, degree).convert(
        kind=np.polynomial.Polynomial
    )
    return [float(v) for v in fit(np.sin(np.pi * x) / x).coef], [
        float(v) for v in fit(np.cos(np.pi * x)).coef
    ]


def split3(x):
    hi = x.astype(bf16).astype(f32)
    rest = x - hi
    mid = rest.astype(bf16).astype(f32)
    return hi, mid, rest - mid


def echoes(data, base, bins, trig):
    where, re_amp, im_amp, rel = (data[j : j + 1] for j in range(4))
    re2, im2 = 2.0 * re_amp, 2.0 * im_amp
    inverse = 0.5 / (rel + (base.astype(f32) + NEAR))
    gain = inverse * -64.0
    bend = inverse * (1.0 / 64.0)
    width = data.shape[1]
    rows = lax.broadcasted_iota(jnp.int32, (bins, width), 0).astype(f32)
    hot = jnp.where(rows == rel, 1.0, 0.0).astype(bf16)
    hot = jnp.concatenate([hot, hot], 1)
    for q in range(P_SIZE // 128):
        parts = [[], []]
        for p in range(0, 128, 16):
            ids = lax.broadcasted_iota(jnp.int32, (16, width), 0)
            along = (ids + (q * 128 + p - P_SIZE // 2)).astype(f32) * SPACING
            offset = along - where
            t = offset * offset * gain
            y = t * bend
            t = t * (1.0 + y * (1.0 + 2.0 * y))
            r = t - jnp.round(t)
            u = r * r
            sn = r * horner(u, trig[0])
            cs = horner(u, trig[1])
            re = re_amp - sn * (re2 * sn + im2 * cs)
            im = im_amp + sn * (re2 * cs - im2 * sn)
            for c, v in enumerate((re, im)):
                parts[c].append(jnp.concatenate(split(v), 1))
        for c in range(2):
            lanes = slice(c * P_SIZE + q * 128, c * P_SIZE + (q + 1) * 128)
            yield lanes, product(hot, jnp.concatenate(parts[c], 0), ((1,), (1,)))


def range_bin_kernel(base_ref, *refs, span, trig):
    out, lead = refs[6:8]
    buf, load = refs[14:]
    cells8, bounce8, pos, amp, cells, bnc = refs[8:14]
    loads = [
        pltpu.make_async_copy(src, dst, load.at[i])
        for i, (src, dst) in enumerate(zip(refs[:6], refs[8:14]))
    ]
    for copy in loads:
        copy.start()
    for copy in loads:
        copy.wait()
    base = base_ref[0]
    rows = cells8.shape[0]
    chunks = rows // 8
    target = cells8[...] + SHIFT * bounce8[...] - base
    match = jnp.where((target >= 0) & (target < span), 1.0, 0.0)
    mb = match.astype(bf16)
    a = lax.broadcasted_iota(jnp.int32, (128, 128), 0)
    b = lax.broadcasted_iota(jnp.int32, (128, 128), 1)
    upto = jnp.where(a <= b, 1.0, 0.0).astype(bf16)
    count = jnp.dot(mb, upto, preferred_element_type=f32)
    total = jnp.dot(mb, jnp.ones((128, 128), bf16), preferred_element_type=f32)
    a = lax.broadcasted_iota(jnp.int32, (rows, rows), 0)
    b = lax.broadcasted_iota(jnp.int32, (rows, rows), 1)
    below = jnp.where((a // 8 == b // 8) & (b < a), 1.0, 0.0).astype(bf16)
    ahead = jnp.dot(below, total.astype(bf16), preferred_element_type=f32)
    rank = jnp.where(match > 0.0, count + ahead - 1.0, -1.0)
    counts = [
        jnp.sum(match[8 * c : 8 * c + 8]).astype(jnp.int32) for c in range(chunks)
    ]

    def values(c):
        lanes = slice(CHUNK * c, CHUNK * (c + 1))
        flip = 1.0 - 2.0 * bnc[:, lanes].astype(f32)
        rel = (cells[:, lanes] + SHIFT * bnc[:, lanes] - base).astype(f32)
        zero = jnp.zeros_like(rel)
        data = jnp.concatenate(
            [pos[:, lanes], amp[0:1, lanes] * flip, amp[1:2, lanes] * flip, rel] + [zero] * 4, 0
        )
        return jnp.concatenate(list(split3(data)) + [jnp.zeros_like(data)], 0).astype(bf16)

    def pick(c, first):
        slots = lax.broadcasted_iota(jnp.int32, (SLOTS, 128), 0).astype(f32) + first
        hot = jnp.concatenate(
            [jnp.where(rank[8 * c + j : 8 * c + j + 1] == slots, 1.0, 0.0) for j in range(8)], 1
        ).astype(bf16)
        return lax.dot_general(
            hot, values(c), (((1,), (1,)), ((), ())), preferred_element_type=f32
        )

    start = 0
    for c in range(chunks):
        buf[pl.ds(start, SLOTS), 0:32] = pick(c, 0.0)
        start = start + counts[c]
    most = functools.reduce(jnp.maximum, counts)

    @pl.when(most > SLOTS)
    def _():
        begin = 0
        for c in range(chunks):

            @pl.loop(0, (counts[c] + SLOTS - 1) // SLOTS)
            def _(i):
                first = (i * SLOTS).astype(f32)
                buf[pl.ds(begin + i * SLOTS, SLOTS), 0:32] = pick(c, first)

            begin = begin + counts[c]

    buf[pl.ds(start, AHEAD), :] = jnp.zeros((AHEAD, 128), f32)

    def data(first, width):
        cols = []
        for h in range(width // 128):
            t = buf[pl.ds(first + h * 128, 128), :].T
            cols.append(t[0:8] + t[8:16] + t[16:24])
        return jnp.concatenate(cols, 1)

    lead[...] = data(0, AHEAD)
    out[...] = jnp.zeros_like(out)

    @pl.loop(AHEAD // WIDE, (start + WIDE - 1) // WIDE)
    def _(i):
        for lanes, sums in echoes(data(i * WIDE, WIDE), base, span, trig):
            out[:, lanes] += sums


def range_binning(positions, amplitude, cells, bounce, base, span):
    count = positions.shape[0]
    rows = count // 128
    sources = (
        cells.reshape(rows, 128),
        bounce.reshape(rows, 128),
        positions.reshape(1, count),
        amplitude,
        cells.reshape(1, count),
        bounce.reshape(1, count),
    )
    return pl.pallas_call(
        functools.partial(range_bin_kernel, span=span, trig=range_trig_coefs(4)),
        in_specs=[pl.BlockSpec(memory_space=pltpu.SMEM)] + [IN_HBM] * len(sources),
        out_specs=(IN_VMEM, IN_VMEM),
        out_shape=(
            jax.ShapeDtypeStruct((span, 2 * P_SIZE), f32),
            jax.ShapeDtypeStruct((8, AHEAD), f32),
        ),
        scratch_shapes=[pltpu.VMEM(a.shape, a.dtype) for a in sources]
        + [
            pltpu.VMEM((count + SLOTS + AHEAD, 128), f32),
            pltpu.SemaphoreType.DMA((len(sources),)),
        ],
        compiler_params=pltpu.CompilerParams(vmem_limit_bytes=16 << 20),
        name="range_binning",
    )(base.reshape(1), *in_hbm(sources))


def complex_rows(c, s):
    return np.block([[c, s], [-s, c]])


def mid_factors(n_dev, order):
    side = np.arange(BIN_SIDE)
    t = np.arange(STOLT)
    eye = np.eye(GROUP)
    a = -2 * np.pi / STOLT * ((side[:, None] * t[None, :]) % STOLT)
    ta = complex_rows(np.cos(a), np.sin(a))[order]
    a = -2 * np.pi / F_LEN * (side[:, None] * t[None, :])
    wa = np.stack([np.tile(np.cos(a), (GROUP, 1)), np.tile(np.sin(a), (GROUP, 1))])
    a = -2 * np.pi / BIN_SIDE * ((side[:, None] * side[None, :]) % BIN_SIDE)
    c, s = np.kron(eye, np.cos(a)), np.kron(eye, np.sin(a))
    tb = complex_rows(c, s).T
    blk = np.arange(BLOCKS)
    a = 2 * np.pi / BLOCKS * ((blk[:, None] * blk[None, :]) % BLOCKS)
    c, s = np.kron(eye, np.cos(a)), np.kron(eye, np.sin(a))
    tc = complex_rows(c, s)
    a = 2 * np.pi / F_LEN * (t[:, None] * blk[None, :])
    wc = np.stack([np.tile(np.cos(a), (1, GROUP)), np.tile(np.sin(a), (1, GROUP))])
    a = 2 * np.pi / STOLT * ((t[:, None] * t[None, :]) % STOLT)
    td = complex_rows(np.cos(a), np.sin(a)).T / F_LEN
    td = td.reshape(2, n_dev, STOLT // n_dev, 2 * STOLT).transpose(1, 0, 2, 3)
    return ta, wa.astype(np.float32), tb, tc, wc.astype(np.float32), td


def mid_tables(n_dev, order):
    ta, wa, tb, tc, wc, td = mid_factors(n_dev, order)
    td = td.reshape(2 * STOLT, 2 * STOLT)
    return np_split(ta), wa, np_split(tb), np_split(tc), wc, np_split(td)


def core_tables(n_dev, order):
    ta, wa, tb, tc, wc, td = mid_factors(n_dev, order)
    td = td.reshape(n_dev, 2, -1, GROUP, 2 * STOLT).transpose(0, 2, 1, 3, 4)
    td = td.reshape(2 * STOLT, 2 * STOLT)
    forward, inverse = quarter_tables()
    return (
        np_split(forward),
        np_split(ta),
        wa,
        np_split(tb),
        np_split(tc),
        wc,
        np_split(td),
    ), np_split(inverse)


def mid_kernel(
    x, cos_p, sin_p, hot, kind, bank_hi, bank_lo, ta, wa, tb, tc, wc, td, out, xs, os, *, subs
):
    n = GROUP * BLOCKS
    step = pl.program_id(0)
    groups = x.shape[1]

    @pl.when(step == 0)
    def _():
        for g in range(groups):
            xs[g] = x[:, g, :]

    parts_hi, parts_lo = [], []
    for g in range(subs):
        lanes = slice(g * n, (g + 1) * n)
        y = dots(split(xs[step * subs + g]), (ta[0], ta[1]), ((0,), (0,)))
        yr, yi = y[:, :STOLT], y[:, STOLT:]
        y = jnp.concatenate([yr * wa[0] - yi * wa[1], yr * wa[1] + yi * wa[0]], 0)
        z = dots((tb[0], tb[1]), split(y), ((1,), (0,)))
        zr, zi = z[:n], z[n:]
        cp, sp = cos_p[lanes], sin_p[lanes]
        z = jnp.concatenate([zr * cp - zi * sp, zr * sp + zi * cp], 1)
        hi, lo = split(z)
        picked = jnp.dot(
            hot[g], jnp.concatenate([hi, lo], 1), preferred_element_type=f32
        ).astype(bf16)
        first, second = picked[:n], picked[n:]
        for c in range(2):
            for base, keep in ((0, parts_hi), (2 * STOLT, parts_lo)):
                cut = slice(base + c * STOLT, base + (c + 1) * STOLT)
                keep.append(jnp.concatenate([first[:, cut], second[:, cut]], 1))
    ghi = jnp.concatenate(parts_hi, 0)
    glo = jnp.concatenate(parts_lo, 0)
    kinds = kind[...].reshape(subs * 2 * n, 1)
    kinds = jnp.broadcast_to(kinds, (subs * 2 * n, STOLT))
    acc = jnp.zeros((subs * 2 * n, STOLT), f32)
    for k in range(0, bank_hi.shape[0], 2):
        khi = jnp.concatenate([bank_hi[k], bank_hi[k + 1]], 1)
        klo = jnp.concatenate([bank_lo[k], bank_lo[k + 1]], 1)
        r = dots((ghi, glo), (khi, klo), ((1,), (0,)))
        for half in range(2):
            acc = jnp.where(kinds == k + half, r[:, half * STOLT : (half + 1) * STOLT], acc)
    for g in range(subs):
        s = acc[g * 2 * n : (g + 1) * 2 * n]
        y = dots(split(s), (tc[0], tc[1]), ((0,), (0,)))
        yr, yi = y[:, :n], y[:, n:]
        y = jnp.concatenate([yr * wc[0] - yi * wc[1], yr * wc[1] + yi * wc[0]], 0)
        os[step * subs + g] = dots((td[0], td[1]), split(y), ((1,), (0,)))

    @pl.when(step == pl.num_programs(0) - 1)
    def _():
        for g in range(groups):
            out[:, g, :] = os[g]


def middle(x, cos_p, sin_p, hot, kind, bank_hi, bank_lo, tables):
    groups = x.shape[1]
    subs = min(4, groups)
    n = GROUP * BLOCKS
    whole = lambda a: pl.BlockSpec(a.shape, lambda i: (0,) * a.ndim)
    return pl.pallas_call(
        functools.partial(mid_kernel, subs=subs),
        grid=(groups // subs,),
        in_specs=[
            whole(x),
            pl.BlockSpec((subs * n, STOLT), lambda i: (i, 0)),
            pl.BlockSpec((subs * n, STOLT), lambda i: (i, 0)),
            pl.BlockSpec((subs, 2 * n, n), lambda i: (i, 0, 0)),
            pl.BlockSpec((subs, 2 * n, 1), lambda i: (i, 0, 0)),
            whole(bank_hi),
            whole(bank_lo),
        ]
        + [whole(t) for t in tables],
        out_specs=pl.BlockSpec((2 * STOLT, groups, n), lambda i: (0, 0, 0)),
        out_shape=jax.ShapeDtypeStruct((2 * STOLT, groups, n), f32),
        scratch_shapes=[
            pltpu.VMEM((groups, x.shape[0], n), f32),
            pltpu.VMEM((groups, 2 * STOLT, n), f32),
        ],
        name="middle",
    )(x, cos_p, sin_p, hot, kind, bank_hi, bank_lo, *tables)


def quarter_tables():
    q = P_SIZE // 4
    m = np.arange(q)
    fwd, inv = [], []
    for low in range(4):
        a = 2 * np.pi / P_SIZE * (((4 * m[:, None] + low) * m[None, :]) % P_SIZE)
        turn = a.reshape(-1, 2, q).transpose(1, 0, 2).reshape(q, q)
        fwd.append(np.concatenate([np.cos(turn), np.sin(turn)], 0))
        inv.append(np.concatenate([np.cos(a.T), np.sin(a.T)], 0) / P_SIZE)
    return np.stack(fwd), np.stack(inv)


def swap_blocks(arrays):
    count = len(arrays)
    lanes = arrays[0].shape[-1]
    size = lanes // count
    block = lax.broadcasted_iota(jnp.int32, arrays[0].shape, 1) // size
    outs = []
    for b in range(count):
        acc = None
        for a in range(count):
            shift = (a - b) % count * size
            moved = pltpu.roll(arrays[a], shift, 1) if shift else arrays[a]
            acc = moved if acc is None else jnp.where(block == a, moved, acc)
        outs.append(acc)
    return outs


def core_kernel(*refs, n_pulse, n_scat, subs, trig, trig_low):
    lead, partial = refs[:2]
    sources = refs[2:12]
    out = refs[12]
    local = refs[13:23]
    steps_in, kinds_in, bank, table, ta, wa, tb, tc, wc, td = local
    binned, peer, spec, x, hot, kind, banks, os = refs[23:31]
    (
        load, own_store, pair_send, pair_recv, near_send, near_recv, far_send, far_recv,
    ) = refs[31:]
    n_dev = n_pulse * n_scat
    pulse = lax.axis_index("pulse")
    scat = lax.axis_index("scat")
    me = pulse * n_scat + scat
    half = peer.shape[0]
    lanes = 2 * half
    size = P_SIZE // 4
    n = GROUP * BLOCKS
    groups = os.shape[1]
    pieces = groups // subs
    quads = lanes // BIN_SIDE
    unit = subs * quads
    per = os.shape[2]
    moves = [(a, b) for a in range(n_pulse) for b in range(n_scat) if (a, b) != (0, 0)]
    moves.sort(key=lambda m: (-min(m[0], n_pulse - m[0]), m))

    def other(a, b):
        return lax.rem(pulse + a, n_pulse), lax.rem(scat + b, n_scat)

    barrier = pltpu.get_barrier_semaphore()
    for a, b in moves:
        p, c = other(a, b)
        pl.semaphore_signal(
            barrier, inc=1, device_id={"pulse": p, "scat": c}, device_id_type=MESH
        )
    keep = pl.ds(pl.multiple_of(scat * half, half), half)
    give = pl.ds(pl.multiple_of((1 - scat) * half, half), half)
    loads = [
        pltpu.make_async_copy(src, dst, load.at[i])
        for i, (src, dst) in enumerate(zip(sources, local))
    ]
    for copy in loads:
        copy.start()
    for cut, sums in echoes(lead[...], pulse * 2 * half, 2 * half, trig_low):
        binned[:, cut] = partial[:, cut] + sums
    pl.semaphore_wait(barrier, n_dev - 1)

    pair = pltpu.make_async_remote_copy(
        src_ref=binned.at[give, :],
        dst_ref=peer,
        send_sem=pair_send,
        recv_sem=pair_recv,
        device_id={"pulse": pulse, "scat": 1 - scat},
        device_id_type=MESH,
    )
    pair.start()
    loads[3].wait()
    pair.wait()

    quarters = []
    for q in range(4):
        pair_of = []
        for c in range(2):
            cut = slice(c * P_SIZE + q * size, c * P_SIZE + (q + 1) * size)
            pair_of.append(binned[keep, cut] + peer[:, cut])
        quarters.append(pair_of)
    (r0, i0), (r1, i1), (r2, i2), (r3, i3) = quarters
    sr, si, dr, di = r0 + r2, i0 + i2, r0 - r2, i0 - i2
    tr, ti, er, ei = r1 + r3, i1 + i3, r1 - r3, i1 - i3
    mixed = (
        (sr + tr, si + ti),
        (dr + ei, di - er),
        (sr - tr, si - ti),
        (dr - ei, di + er),
    )
    low = lax.broadcasted_iota(jnp.int32, (size, lanes), 1) < half
    rows = []
    for k in range(4):
        g = product(
            joined(table[0, k], table[1, k], 1),
            triple(jnp.concatenate(mixed[k], 0), 1),
            ((1,), (1,)),
        )
        turned = pltpu.roll(g[size:], half, 1)
        rows.append(g[:size] + jnp.where(low, turned, -turned))
    for q, z in enumerate(swap_blocks(rows)):
        for h in range(subs):
            spec[pl.ds(q * subs + h, size // subs, stride=unit), :] = z[
                h * (size // subs) : (h + 1) * (size // subs)
            ]

    def piece(dev, i):
        return pl.ds(pl.multiple_of((dev * pieces + i) * unit, unit), unit)

    own = pl.ds(pl.multiple_of(me * unit, unit), unit)
    for i in range(pieces):
        for j, (a, b) in enumerate(moves):
            p, c = other(a, b)
            pltpu.make_async_remote_copy(
                src_ref=spec.at[piece(p * n_scat + c, i), :],
                dst_ref=x.at[i, own, :],
                send_sem=near_send.at[j],
                recv_sem=near_recv.at[i, me],
                device_id={"pulse": p, "scat": c},
                device_id_type=MESH,
            ).start()
    for i in range(pieces):
        x[i, own, :] = spec[piece(me, i), :]

    for i in (0, 1, 2, 4, 5, 6, 7, 8, 9):
        loads[i].wait()
    block = lax.broadcasted_iota(jnp.int32, (n, STOLT), 0)
    lane = lax.broadcasted_iota(jnp.int32, (n, STOLT), 1)
    spot = lane.astype(f32)
    above = (block // BLOCKS * BLOCKS).astype(f32)
    flat = []
    for ref in (steps_in, kinds_in):
        flat.append(
            jnp.concatenate([ref[pl.ds(j, groups, stride=GROUP), :] for j in range(GROUP)], 1)
        )
    for g in range(groups):
        first = jnp.broadcast_to(flat[0][g : g + 1].astype(f32), (n, n)).T + above
        hot[g, :n] = jnp.where(first == spot, 1.0, 0.0).astype(bf16)
        hot[g, n:] = jnp.where(first + 1.0 == spot, 1.0, 0.0).astype(bf16)
        kind[g] = jnp.broadcast_to(flat[1][g : g + 1].astype(f32), (n, n)).T
    for k in range(bank.shape[0]):
        hi, lo = split(bank[k])
        cut = slice(k % 2 * STOLT, (k % 2 + 1) * STOLT)
        banks[k // 2, :, cut] = jnp.concatenate([hi, hi, lo], 0)

    cols = (lane + (block % BLOCKS) * STOLT).astype(f32)
    kr = 4.0 * np.pi / 3e8 * (9.6e9 + (cols - F_LEN // 2) * (1.5e8 / F_LEN))

    def phase(g):
        row = me * (groups * GROUP) + g * GROUP + block // BLOCKS
        centered = lax.rem(row + P_SIZE // 2, P_SIZE) - P_SIZE // 2
        along = 2.0 * np.pi / (P_SIZE * SPACING) * centered.astype(f32)
        squared = along * along
        depth = NEAR + B // 2
        theta = -depth * squared / (jnp.sqrt(kr * kr - squared) + kr)
        whole = jnp.round(theta * (0.5 / np.pi))
        for part in turn_parts():
            theta = theta - whole * part
        r = theta * (0.5 / np.pi)
        u = r * r
        sn = r * horner(u, trig[0])
        cs = horner(u, trig[1])
        return 1.0 - 2.0 * sn * sn, 2.0 * sn * cs

    def ranged(i, h):
        g = i * subs + h
        cp, sp = phase(g)
        rows_in = x[i, pl.ds(h, n_dev * quads, stride=subs), :]
        y = product(triple(rows_in, 0), joined(ta[0], ta[1], 0), ((0,), (0,)))
        yr, yi = y[:, :STOLT], y[:, STOLT:]
        y = jnp.concatenate([yr * wa[0] - yi * wa[1], yr * wa[1] + yi * wa[0]], 0)
        z = product(joined(tb[0], tb[1], 1), triple(y, 0))
        zr, zi = z[:n], z[n:]
        z = jnp.concatenate([zr * cp - zi * sp, zr * sp + zi * cp], 1)
        picked = product(hot[g], jnp.concatenate(split(z), 1)).astype(bf16)
        first, second = picked[:n], picked[n:]
        parts = []
        for base in (0, 2 * STOLT):
            cuts = [slice(base + c * STOLT, base + (c + 1) * STOLT) for c in range(2)]
            parts.append(
                jnp.concatenate(
                    [jnp.concatenate([first[:, v], second[:, v]], 1) for v in cuts], 0
                )
            )
        ghi, glo = parts
        windows = jnp.concatenate([ghi, glo, ghi], 1)
        kinds = jnp.concatenate([kind[g]] * 2, 0)
        acc = jnp.zeros((2 * n, STOLT), f32)
        for k in range(banks.shape[0]):
            r = product(windows, banks[k])
            for v in range(2):
                acc = jnp.where(kinds == 2 * k + v, r[:, v * STOLT : (v + 1) * STOLT], acc)
        y = product(triple(acc, 0), joined(tc[0], tc[1], 0), ((0,), (0,)))
        yr, yi = y[:, :n], y[:, n:]
        y = jnp.concatenate([yr * wc[0] - yi * wc[1], yr * wc[1] + yi * wc[0]], 0)
        z = product(joined(td[0], td[1], 1), triple(y, 0))
        os[:, g] = z.reshape(n_dev, per, n)
        for j, (a, b) in enumerate(moves):
            p, c = other(a, b)
            pltpu.make_async_remote_copy(
                src_ref=os.at[p * n_scat + c, g],
                dst_ref=out.at[me, g],
                send_sem=far_send.at[j],
                recv_sem=far_recv.at[me],
                device_id={"pulse": p, "scat": c},
                device_id_type=MESH,
            ).start()

    def step(i, carry):
        for a, b in moves:
            p, c = other(a, b)
            src = p * n_scat + c
            here = pl.ds(pl.multiple_of(src * unit, unit), unit)
            pltpu.make_async_copy(
                x.at[i, here, :], x.at[i, here, :], near_recv.at[i, src]
            ).wait()
        for h in range(subs):
            ranged(i, h)
        return carry

    lax.fori_loop(0, pieces, step, 0)
    mine = pltpu.make_async_copy(os.at[me], out.at[me], own_store)
    mine.start()
    mine.wait()
    for j, (a, b) in enumerate(moves):
        p, c = other(a, b)
        src = p * n_scat + c
        all_of = spec.at[pl.ds(0, pieces * unit), :]
        pltpu.make_async_copy(all_of, all_of, near_send.at[j]).wait()
        pltpu.make_async_copy(os.at[src], os.at[src], far_send.at[j]).wait()
        pltpu.make_async_copy(out.at[src], out.at[src], far_recv.at[src]).wait()


def turn_parts():
    parts, rest = [], 2.0 * np.pi
    for bits in (10, 22, 60):
        scale = 2.0**bits
        part = float(np.float32(np.round(rest * scale) / scale))
        parts.append(part)
        rest -= part
    return parts


def core(partial, lead, steps_in, kinds_in, bank, tables, n_pulse, n_scat):
    n_dev = n_pulse * n_scat
    groups = steps_in.shape[0] // GROUP
    subs = 2
    n = GROUP * BLOCKS
    span, width = partial.shape
    half = span // n_scat
    quads = 2 * half // BIN_SIDE
    kernels = bank.shape[0]
    per = 2 * STOLT // n_dev
    sources = (steps_in, kinds_in, bank, *tables)
    dma = pltpu.SemaphoreType.DMA
    return pl.pallas_call(
        functools.partial(
            core_kernel,
            n_pulse=n_pulse,
            n_scat=n_scat,
            subs=subs,
            trig=range_trig_coefs(5),
            trig_low=range_trig_coefs(4),
        ),
        in_specs=[IN_VMEM] * 2 + [IN_HBM] * len(sources),
        out_specs=pl.BlockSpec(memory_space=pl.ANY),
        out_shape=jax.ShapeDtypeStruct((n_dev, groups, per, n), f32),
        scratch_shapes=[pltpu.VMEM(a.shape, a.dtype) for a in sources]
        + [
            pltpu.VMEM((span, width), f32),
            pltpu.VMEM((half, width), f32),
            pltpu.VMEM((n_dev * groups * quads, n), f32),
            pltpu.VMEM((groups // subs, n_dev * subs * quads, n), f32),
            pltpu.VMEM((groups, 2 * n, n), bf16),
            pltpu.VMEM((groups, n, STOLT), f32),
            pltpu.VMEM((kernels // 2, 6 * STOLT, 2 * STOLT), bf16),
            pltpu.VMEM((n_dev, groups, per, n), f32),
            dma((len(sources),)),
            dma,
            dma,
            dma,
            dma((n_dev,)),
            dma((groups // subs, n_dev)),
            dma((n_dev,)),
            dma((n_dev,)),
        ],
        compiler_params=pltpu.CompilerParams(
            collective_id=0, has_side_effects=True, vmem_limit_bytes=24 << 20
        ),
        name="core",
    )(lead, partial, *in_hbm(sources))


def image_kernel(x, table, out, done, sems):
    devs, kh, per, lanes = x.shape
    size = P_SIZE // 4
    copies = []
    for h in range(per // (2 * GROUP)):
        columns = [[] for _ in range(4)]
        for c in range(2):
            first = (2 * h + c) * GROUP
            tiles = [x[:, :, first + j, :].reshape(devs * kh, lanes) for j in range(4)]
            for k, z in enumerate(swap_blocks(tiles)):
                columns[k].append(z)
        v = []
        for k in range(4):
            g = product(
                joined(table[0, k], table[1, k], 1), triple(jnp.concatenate(columns[k], 1), 0)
            )
            cos_g, sin_g = g[:size], g[size:]
            v.append((cos_g[:, :lanes] - sin_g[:, lanes:], cos_g[:, lanes:] + sin_g[:, :lanes]))
        (r0, i0), (r1, i1), (r2, i2), (r3, i3) = v
        sr, si, dr, di = r0 + r2, i0 + i2, r0 - r2, i0 - i2
        tr, ti, er, ei = r1 + r3, i1 + i3, r1 - r3, i1 - i3
        mixed = (
            (sr + tr, si + ti),
            (dr - ei, di + er),
            (sr - tr, si - ti),
            (dr + ei, di - er),
        )
        for q in range(4):
            for c in range(2):
                done[h, c, q * size : (q + 1) * size, :] = mixed[q][c]
        copy = pltpu.make_async_copy(
            done.at[h], out.at[:, :, pl.ds(h * lanes, lanes)], sems.at[h]
        )
        copy.start()
        copies.append(copy)
    for copy in copies:
        copy.wait()


def reference_phase(row_ids, cols):
    centered = (row_ids + P_SIZE // 2) % P_SIZE - P_SIZE // 2
    along_k = 2.0 * jnp.pi / (P_SIZE * SPACING) * centered.astype(f32)
    kr = 4.0 * jnp.pi / 3e8 * (9.6e9 + (cols.astype(f32) - F_LEN // 2) * (1.5e8 / F_LEN))
    squared = along_k * along_k
    depth = NEAR + B // 2
    return (
        -depth
        * squared[:, None]
        / (jnp.sqrt(kr[None, :] * kr[None, :] - squared[:, None]) + kr[None, :])
    )


def on_device(positions, amplitude, range_cells, bounce, stolt_block, kernel_choice, kernel_bank):
    n_pulse = lax.axis_size("pulse")
    n_scat = lax.axis_size("scat")
    n_dev = n_pulse * n_scat
    pulse_here = lax.axis_index("pulse")
    scat_here = lax.axis_index("scat")
    pulses = P_SIZE // n_pulse
    rows = P_SIZE // n_dev
    width = F_LEN // n_dev
    groups = rows // GROUP
    n = GROUP * BLOCKS
    bins_scat = B // n_scat
    bins_here = bins_scat // n_pulse

    per = STOLT // n_dev
    span = B // n_pulse
    packed = (
        span == 128
        and n_scat == 2
        and per % 4 == 0
        and groups % 8 == 0
        and positions.shape[0] % CHUNK == 0
    )
    if packed:
        partial, lead = range_binning(
            positions, amplitude, range_cells, bounce, pulse_here * span, span
        )
        local = bins_here // BIN_SIDE
        i, s, c, l = np.meshgrid(
            np.arange(n_pulse), np.arange(n_scat), np.arange(2), np.arange(local), indexing="ij"
        )
        order = (c * BIN_SIDE + (i * n_scat + s) * local + l).reshape(-1)
        tables, backward = core_tables(n_dev, order)
        tables = tuple(jnp.asarray(t) for t in tables)
        columns = core(
            partial, lead, stolt_block, kernel_choice, kernel_bank, tables, n_pulse, n_scat
        )
        return pl.pallas_call(
            image_kernel,
            in_specs=[IN_VMEM, IN_VMEM],
            out_specs=pl.BlockSpec(memory_space=pl.ANY),
            out_shape=jax.ShapeDtypeStruct((2, P_SIZE, width), f32),
            scratch_shapes=[
                pltpu.VMEM((width // n, 2, P_SIZE, n), f32),
                pltpu.SemaphoreType.DMA((width // n,)),
            ],
            compiler_params=pltpu.CompilerParams(vmem_limit_bytes=16 << 20),
            name="image",
        )(columns, jnp.asarray(backward))

    ids = jnp.arange(GROUP, dtype=jnp.int32)[None, :, None] * BLOCKS
    first = stolt_block.reshape(groups, GROUP, BLOCKS) + ids
    pick = jnp.stack([first, first + 1], 1).reshape(groups, 2 * n, 1)
    hot = (pick == jnp.arange(n, dtype=jnp.int32)[None, None, :]).astype(bf16)
    kind = jnp.stack([kernel_choice.reshape(groups, n)] * 2, 1).reshape(groups, 2 * n, 1)
    bank_hi = lax.reduce_precision(kernel_bank, 8, 7)
    bank_lo = (kernel_bank - bank_hi).astype(bf16)
    bank_hi = bank_hi.astype(bf16)
    row_ids = (pulse_here * n_scat + scat_here) * rows + jnp.arange(rows, dtype=jnp.int32)
    theta = reference_phase(row_ids, jnp.arange(F_LEN, dtype=jnp.int32))
    theta = theta.reshape(rows * BLOCKS, STOLT)
    cos_p, sin_p = jnp.cos(theta), jnp.sin(theta)

    partial = binning(positions, amplitude, range_cells, bounce, pulse_here * pulses, pulses)
    partial = partial.reshape(n_scat, bins_scat, 2 * pulses)
    binned = lax.dynamic_index_in_dim(partial, scat_here, 0, keepdims=False)
    for shift in range(1, n_scat):
        other = lax.dynamic_index_in_dim(
            partial, (scat_here + shift) % n_scat, 0, keepdims=False
        )
        ring = [(i, (i + shift) % n_scat) for i in range(n_scat)]
        binned = binned + lax.ppermute(other, "scat", ring)
    turned = lax.all_to_all(
        binned.reshape(n_pulse, bins_here, 2 * pulses), "pulse", 0, 0, tiled=True
    )
    turned = turned.reshape(n_pulse, bins_here, 2, pulses).transpose(0, 3, 2, 1)
    turned = turned.reshape(P_SIZE, 2 * bins_here)
    k = np.arange(P_SIZE)
    angle = 2 * np.pi / P_SIZE * ((k[:, None] * k[None, :]) % P_SIZE)
    az = jnp.asarray(np.concatenate([np.cos(angle), np.sin(angle)], 0), f32)
    product = jnp.dot(az, turned, precision=HIGH, preferred_element_type=f32)
    pc, ps = product[:P_SIZE], product[P_SIZE:]
    spectrum = pc + jnp.concatenate([ps[:, bins_here:], -ps[:, :bins_here]], 1)
    az_rows = lax.all_to_all(
        spectrum.reshape(n_dev, rows, 2 * bins_here), ("pulse", "scat"), 0, 0, tiled=True
    )
    x = az_rows.reshape(n_pulse, n_scat, rows, 2, bins_here).transpose(3, 1, 0, 4, 2)
    x = x.reshape(2, BIN_SIDE, BIN_SIDE, rows).transpose(0, 1, 3, 2)
    x = x.reshape(2 * BIN_SIDE, groups, n)
    order = np.arange(2 * BIN_SIDE)

    tables = tuple(jnp.asarray(t) for t in mid_tables(n_dev, order))
    ranged = middle(x, cos_p, sin_p, hot, kind, bank_hi, bank_lo, tables)
    columns = lax.all_to_all(
        ranged.reshape(n_dev, 2 * per, rows * BLOCKS), ("pulse", "scat"), 0, 0, tiled=True
    )
    columns = columns.reshape(n_dev, 2, per, rows, BLOCKS).transpose(0, 3, 1, 2, 4)
    columns = columns.reshape(P_SIZE, 2 * width)
    final = jnp.dot(az, columns, precision=HIGH, preferred_element_type=f32)
    fc, fs = final[:P_SIZE], final[P_SIZE:]
    re = (fc[:, :width] - fs[:, width:]) / P_SIZE
    im = (fc[:, width:] + fs[:, :width]) / P_SIZE
    return jnp.stack([re, im])


def solution(mesh):
    placed = (
        P(("scene", "scat")),
        P(None, ("scene", "scat")),
        P(("scene", "scat")),
        P(("scene", "scat")),
        P(("pulse", "scat"), None),
        P(("pulse", "scat"), None),
        P(),
    )
    return jax.shard_map(
        on_device,
        mesh=mesh,
        in_specs=placed,
        out_specs=P(None, "scene", ("pulse", "scat")),
        check_vma=False,
    )
```

profile of v0, /device:TPU:0, one launch (start us, length us, event | category | flops | bytes accessed | tf_op | source)
XLA Modules:
  0.0 47.1 jit_solution(6811425674861744658)
XLA Ops:
  0.0 2.6 %range_binning.1 = (f32[128,1024]{1,0:T(8,128)S(1)}, f32[8,1024]{1,0:T(8,128)S(1)}) custom-call(s32[1]{0:T(128)} %bitcast.base_ref, s32[64,128]{1,0:T(8,128)} %bitcast.6, s32[64,128]{1,0:T(8,128)} %bitcast.8, f32[1,8192]{1,0:T(1,128)} %bitcast.10, f32[2,8192]{1,0:T(2,128)} %refs_3_.2, s32[1,8192]{1,0:T(1,128)} %bitcast.7, s32[1,8192]{1,0:T(1,128)} %bitcast.9), custom_call_target="tpu_custom_call" | custom-call | tf_op jit(solution)/shard_map/range_binning/pallas_call | solution.py:302
  2.6 0.0 copy-start
  2.7 42.0 %core.1.x = f32[16,8,16,128]{3,2,1,0:T(8,128)S(1)} custom-call(f32[8,1024]{1,0:T(8,128)S(1)} %get-tuple-element.7.refs_0_, f32[128,1024]{1,0:T(8,128)S(1)} %get-tuple-element.8.refs_1_, s32[32,32]{1,0:T(8,128)} %refs_2_.1, s32[32,32]{1,0:T(8,128)} %refs_3_.3, f32[16,256,128]{2,1,0:T(8,128)} %refs_4_.1, bf16[2,4,256,128]{3,2,1,0:T(8,128)(2,1)} %constant.22.clone.refs_5_, ...), custom_call_target="tpu_custom_call" | custom-call | tf_op jit(solution)/shard_map/core/pallas_call | solution.py:720
  44.6 0.0 copy-done
  44.6 2.3 %image.1 = f32[2,512,256]{2,1,0:T(8,128)} custom-call(f32[16,8,16,128]{3,2,1,0:T(8,128)S(1)} %core.1.x, bf16[2,4,256,128]{3,2,1,0:T(8,128)(2,1)S(1)} %copy-done), custom_call_target="tpu_custom_call" | custom-call | tf_op jit(solution)/shard_map/image/pallas_call | solution.py:847
Async XLA Ops:
  2.6 42.0 %copy-start = (bf16[2,4,256,128]{3,2,1,0:T(8,128)(2,1)S(1)}, bf16[2,4,256,128]{3,2,1,0:T(8,128)(2,1)}, u32[]{:S(2)}) copy-start(bf16[2,4,256,128]{3,2,1,0:T(8,128)(2,1)} %constant.28.clone.table) | copy-start | bytes 1572868
where the time goes:
time: 47.2 us; the launch traced here: 47.1 us
  Pallas kernels  46.9 us (99%)
    pallas_call x1, Pallas kernels, core(): pl.pallas_call(functools.partial(core_kernel, n_pulse=n_pulse, n_scat=n_s...  42 us
    pallas_call x1, Pallas kernels, range_binning(): pl.pallas_call(functools.partial(range_bin_kernel, span=span, trig=range_...  2.64 us
    pallas_call x1, Pallas kernels, on_device(): pl.pallas_call(image_kernel, in_specs=[IN_VMEM, IN_VMEM], out_specs=pl.Bl...  2.28 us

commit v1 on v0

--- a/solution.py
+++ b/solution.py
@@ -22,6 +22,8 @@
 SLOTS = 192
 WIDE = 128
 AHEAD = 1024
+SHARED = 1
+STREAM = 512
 HIGH = lax.Precision.HIGH
 MESH = pl.DeviceIdType.MESH
 IN_HBM = pl.BlockSpec(memory_space=pltpu.HBM)
@@ -483,10 +485,11 @@
     out = refs[12]
     local = refs[13:23]
     steps_in, kinds_in, bank, table, ta, wa, tb, tc, wc, td = local
-    binned, peer, spec, x, hot, kind, banks, os = refs[23:31]
+    binned, peer, spec, x, hot, kind, banks, os, twin_os, *twin_in = refs[23:34]
     (
         load, own_store, pair_send, pair_recv, near_send, near_recv, far_send, far_recv,
-    ) = refs[31:]
+        twin_send, twin_recv, half_send,
+    ) = refs[34:]
     n_dev = n_pulse * n_scat
     pulse = lax.axis_index("pulse")
     scat = lax.axis_index("scat")
@@ -495,8 +498,11 @@
     lanes = 2 * half
     size = P_SIZE // 4
     n = GROUP * BLOCKS
-    groups = os.shape[1]
+    groups = os.shape[1] + SHARED
     pieces = groups // subs
+    reach = n_pulse // 2
+    side = lax.div(pulse, reach)
+    twin = lax.rem(pulse + reach, n_pulse) * n_scat + scat
     quads = lanes // BIN_SIDE
     unit = subs * quads
     per = os.shape[2]
@@ -533,6 +539,19 @@
         device_id_type=MESH,
     )
     pair.start()
+    metas = []
+    for i in range(2):
+        loads[i].wait()
+        copy = pltpu.make_async_remote_copy(
+            src_ref=local[i],
+            dst_ref=twin_in[i],
+            send_sem=twin_send.at[i],
+            recv_sem=twin_recv.at[i],
+            device_id={"pulse": lax.rem(pulse + reach, n_pulse), "scat": scat},
+            device_id_type=MESH,
+        )
+        copy.start()
+        metas.append(copy)
     loads[3].wait()
     pair.wait()
 
@@ -571,47 +590,56 @@
     def piece(dev, i):
         return pl.ds(pl.multiple_of((dev * pieces + i) * unit, unit), unit)
 
+    def source(p, c, i):
+        if i < pieces:
+            return piece(p * n_scat + c, i)
+        return piece(lax.rem(p + reach, n_pulse) * n_scat + c, pieces - 1)
+
     own = pl.ds(pl.multiple_of(me * unit, unit), unit)
-    for i in range(pieces):
+    for i in range(pieces + 1):
         for j, (a, b) in enumerate(moves):
             p, c = other(a, b)
             pltpu.make_async_remote_copy(
-                src_ref=spec.at[piece(p * n_scat + c, i), :],
+                src_ref=spec.at[source(p, c, i), :],
                 dst_ref=x.at[i, own, :],
                 send_sem=near_send.at[j],
                 recv_sem=near_recv.at[i, me],
                 device_id={"pulse": p, "scat": c},
                 device_id_type=MESH,
             ).start()
-    for i in range(pieces):
-        x[i, own, :] = spec[piece(me, i), :]
-
-    for i in (0, 1, 2, 4, 5, 6, 7, 8, 9):
+    for i in range(pieces + 1):
+        x[i, own, :] = spec[source(pulse, scat, i), :]
+
+    for i in (2, 4, 5, 6, 7, 8, 9):
         loads[i].wait()
+    for copy in metas:
+        copy.wait()
     block = lax.broadcasted_iota(jnp.int32, (n, STOLT), 0)
     lane = lax.broadcasted_iota(jnp.int32, (n, STOLT), 1)
     spot = lane.astype(f32)
     above = (block // BLOCKS * BLOCKS).astype(f32)
     flat = []
-    for ref in (steps_in, kinds_in):
-        flat.append(
+    for i in range(2):
+        both = [
             jnp.concatenate([ref[pl.ds(j, groups, stride=GROUP), :] for j in range(GROUP)], 1)
-        )
-    for g in range(groups):
+            for ref in (local[i], twin_in[i])
+        ]
+        flat.append(jnp.concatenate([both[0], both[1][groups - subs :]], 0))
+    for g in range(groups + subs):
         first = jnp.broadcast_to(flat[0][g : g + 1].astype(f32), (n, n)).T + above
         hot[g, :n] = jnp.where(first == spot, 1.0, 0.0).astype(bf16)
         hot[g, n:] = jnp.where(first + 1.0 == spot, 1.0, 0.0).astype(bf16)
-        kind[g] = jnp.broadcast_to(flat[1][g : g + 1].astype(f32), (n, n)).T
+        kind[g] = jnp.broadcast_to(flat[1][g : g + 1], (8, n))
     for k in range(bank.shape[0]):
-        hi, lo = split(bank[k])
-        cut = slice(k % 2 * STOLT, (k % 2 + 1) * STOLT)
-        banks[k // 2, :, cut] = jnp.concatenate([hi, hi, lo], 0)
+        turned = jnp.concatenate([bank[k, :STOLT].T, bank[k, STOLT:].T], 1)
+        hi, lo = split(turned)
+        banks[k * STOLT : (k + 1) * STOLT] = jnp.concatenate([hi, hi, lo], 1)
 
     cols = (lane + (block % BLOCKS) * STOLT).astype(f32)
     kr = 4.0 * np.pi / 3e8 * (9.6e9 + (cols - F_LEN // 2) * (1.5e8 / F_LEN))
 
-    def phase(g):
-        row = me * (groups * GROUP) + g * GROUP + block // BLOCKS
+    def phase(owner, g):
+        row = owner * (groups * GROUP) + g * GROUP + block // BLOCKS
         centered = lax.rem(row + P_SIZE // 2, P_SIZE) - P_SIZE // 2
         along = 2.0 * np.pi / (P_SIZE * SPACING) * centered.astype(f32)
         squared = along * along
@@ -626,9 +654,9 @@
         cs = horner(u, trig[1])
         return 1.0 - 2.0 * sn * sn, 2.0 * sn * cs
 
-    def ranged(i, h):
-        g = i * subs + h
-        cp, sp = phase(g)
+    def ranged(slot, owner, g, cut):
+        i, h = lax.div(slot, subs), lax.rem(slot, subs)
+        cp, sp = phase(owner, g)
         rows_in = x[i, pl.ds(h, n_dev * quads, stride=subs), :]
         y = product(triple(rows_in, 0), joined(ta[0], ta[1], 0), ((0,), (0,)))
         yr, yi = y[:, :STOLT], y[:, STOLT:]
@@ -636,7 +664,7 @@
         z = product(joined(tb[0], tb[1], 1), triple(y, 0))
         zr, zi = z[:n], z[n:]
         z = jnp.concatenate([zr * cp - zi * sp, zr * sp + zi * cp], 1)
-        picked = product(hot[g], jnp.concatenate(split(z), 1)).astype(bf16)
+        picked = product(hot[slot], jnp.concatenate(split(z), 1)).astype(bf16)
         first, second = picked[:n], picked[n:]
         parts = []
         for base in (0, 2 * STOLT):
@@ -648,17 +676,34 @@
             )
         ghi, glo = parts
         windows = jnp.concatenate([ghi, glo, ghi], 1)
-        kinds = jnp.concatenate([kind[g]] * 2, 0)
-        acc = jnp.zeros((2 * n, STOLT), f32)
-        for k in range(banks.shape[0]):
-            r = product(windows, banks[k])
-            for v in range(2):
-                acc = jnp.where(kinds == 2 * k + v, r[:, v * STOLT : (v + 1) * STOLT], acc)
-        y = product(triple(acc, 0), joined(tc[0], tc[1], 0), ((0,), (0,)))
+        kinds = jnp.concatenate([kind[slot, 0:1]] * 2, 1)
+        acc = jnp.zeros((STOLT, 2 * n), f32)
+        for first in range(0, banks.shape[0], STREAM):
+            r = product(banks[first : first + STREAM], windows, ((1,), (1,)))
+            for v in range(STREAM // STOLT):
+                k = first // STOLT + v
+                acc = jnp.where(kinds == k, r[v * STOLT : (v + 1) * STOLT], acc)
+        y = product(triple(acc, 1), joined(tc[0], tc[1], 0))
         yr, yi = y[:, :n], y[:, n:]
         y = jnp.concatenate([yr * wc[0] - yi * wc[1], yr * wc[1] + yi * wc[0]], 0)
-        z = product(joined(td[0], td[1], 1), triple(y, 0))
-        os[:, g] = z.reshape(n_dev, per, n)
+        z = product(joined(td[0, cut, :], td[1, cut, :], 1), triple(y, 0))
+        return z.reshape(-1, per, n)
+
+    def arrived(i):
+        for a, b in moves:
+            p, c = other(a, b)
+            src = p * n_scat + c
+            here = pl.ds(pl.multiple_of(src * unit, unit), unit)
+            pltpu.make_async_copy(
+                x.at[i, here, :], x.at[i, here, :], near_recv.at[i, src]
+            ).wait()
+
+    def step(g, carry):
+        @pl.when(lax.rem(g, subs) == 0)
+        def _():
+            arrived(lax.div(g, subs))
+
+        os[:, g] = ranged(g, me, g, slice(None))
         for j, (a, b) in enumerate(moves):
             p, c = other(a, b)
             pltpu.make_async_remote_copy(
@@ -669,30 +714,67 @@
                 device_id={"pulse": p, "scat": c},
                 device_id_type=MESH,
             ).start()
-
-    def step(i, carry):
-        for a, b in moves:
-            p, c = other(a, b)
-            src = p * n_scat + c
-            here = pl.ds(pl.multiple_of(src * unit, unit), unit)
-            pltpu.make_async_copy(
-                x.at[i, here, :], x.at[i, here, :], near_recv.at[i, src]
-            ).wait()
-        for h in range(subs):
-            ranged(i, h)
         return carry
 
-    lax.fori_loop(0, pieces, step, 0)
-    mine = pltpu.make_async_copy(os.at[me], out.at[me], own_store)
-    mine.start()
-    mine.wait()
+    close = [(a, b) for a in range(reach) for b in range(n_scat) if (a, b) != (0, 0)]
+    within = pulse - side * reach
+
+    def beside(a, b):
+        return lax.rem(within + a, reach), lax.rem(scat + b, n_scat)
+
+    part = 2 * STOLT // 2
+    served = pl.ds(pl.multiple_of(side * part, part), part)
+
+    lax.fori_loop(0, groups - SHARED, step, 0)
+    if SHARED == subs:
+        arrived(pieces - 1)
+    arrived(pieces)
+
+    def half_step(t, carry):
+        v, h = lax.div(t, SHARED), lax.rem(t, SHARED)
+        owner = lax.rem(pulse + v * reach, n_pulse) * n_scat + scat
+        g = groups - SHARED + h
+        twin_os[v, :, h] = ranged(g + v * subs, owner, g, served)
+        for j, (a, b) in enumerate(close):
+            p, c = beside(a, b)
+            pltpu.make_async_remote_copy(
+                src_ref=twin_os.at[v, p * n_scat + c, h],
+                dst_ref=out.at[owner, g],
+                send_sem=half_send.at[j],
+                recv_sem=far_recv.at[owner],
+                device_id={"pulse": side * reach + p, "scat": c},
+                device_id_type=MESH,
+            ).start()
+        return carry
+
+    lax.fori_loop(0, 2 * SHARED, half_step, 0)
+    first, last = pl.ds(0, groups - SHARED), pl.ds(groups - SHARED, SHARED)
+    here = within * n_scat + scat
+    stores = [
+        pltpu.make_async_copy(src, dst, own_store.at[i])
+        for i, (src, dst) in enumerate(
+            (
+                (os.at[me], out.at[me, first]),
+                (twin_os.at[0, here], out.at[me, last]),
+                (twin_os.at[1, here], out.at[twin, last]),
+            )
+        )
+    ]
+    for copy in stores:
+        copy.start()
+    for copy in stores:
+        copy.wait()
+    for j, (a, b) in enumerate(close):
+        whole = os.at[0, pl.ds(0, 2 * SHARED)]
+        pltpu.make_async_copy(whole, whole, half_send.at[j]).wait()
     for j, (a, b) in enumerate(moves):
         p, c = other(a, b)
         src = p * n_scat + c
-        all_of = spec.at[pl.ds(0, pieces * unit), :]
-        pltpu.make_async_copy(all_of, all_of, near_send.at[j]).wait()
+        whole = spec.at[pl.ds(0, (pieces + 1) * unit), :]
+        pltpu.make_async_copy(whole, whole, near_send.at[j]).wait()
         pltpu.make_async_copy(os.at[src], os.at[src], far_send.at[j]).wait()
-        pltpu.make_async_copy(out.at[src], out.at[src], far_recv.at[src]).wait()
+        whole = out.at[src, first] if (a, b) == (reach, 0) else out.at[src]
+        pltpu.make_async_copy(whole, whole, far_recv.at[src]).wait()
 
 
 def turn_parts():
@@ -734,19 +816,25 @@
             pltpu.VMEM((span, width), f32),
             pltpu.VMEM((half, width), f32),
             pltpu.VMEM((n_dev * groups * quads, n), f32),
-            pltpu.VMEM((groups // subs, n_dev * subs * quads, n), f32),
-            pltpu.VMEM((groups, 2 * n, n), bf16),
-            pltpu.VMEM((groups, n, STOLT), f32),
-            pltpu.VMEM((kernels // 2, 6 * STOLT, 2 * STOLT), bf16),
-            pltpu.VMEM((n_dev, groups, per, n), f32),
+            pltpu.VMEM((groups // subs + 1, n_dev * subs * quads, n), f32),
+            pltpu.VMEM((groups + subs, 2 * n, n), bf16),
+            pltpu.VMEM((groups + subs, 8, n), jnp.int32),
+            pltpu.VMEM((kernels * STOLT, 6 * STOLT), bf16),
+            pltpu.VMEM((n_dev, groups - SHARED, per, n), f32),
+            pltpu.VMEM((2, n_dev // 2, SHARED, per, n), f32),
+            pltpu.VMEM(steps_in.shape, steps_in.dtype),
+            pltpu.VMEM(kinds_in.shape, kinds_in.dtype),
             dma((len(sources),)),
-            dma,
+            dma((3,)),
             dma,
             dma,
             dma((n_dev,)),
-            dma((groups // subs, n_dev)),
+            dma((groups // subs + 1, n_dev)),
             dma((n_dev,)),
             dma((n_dev,)),
+            dma((2,)),
+            dma((2,)),
+            dma((n_dev // 2,)),
         ],
         compiler_params=pltpu.CompilerParams(
             collective_id=0, has_side_effects=True, vmem_limit_bytes=24 << 20

time: 47.2 us -> 45.2 us (0.958)
  Pallas kernels: 46.9 us -> 44.7 us
    pallas_call x1, Pallas kernels: 42 us -> 39.1 us  [core(): pl.pallas_call(functools.partial(core_kernel, n_pulse=n_pulse, n_scat=n_s...]
    pallas_call x1, Pallas kernels: 2.64 us -> 3.38 us  [range_binning(): pl.pallas_call(functools.partial(range_bin_kernel, span=span, trig=range_...]
where the time goes in v1:
time: 45.2 us; the launch traced here: 44.9 us
  Pallas kernels  44.7 us (99%)
    pallas_call x1, Pallas kernels, core(): pl.pallas_call(functools.partial(core_kernel, n_pulse=n_pulse, n_scat=n_s...  39.1 us
    pallas_call x1, Pallas kernels, range_binning(): pl.pallas_call(functools.partial(range_bin_kernel, span=span, trig=range_...  3.38 us
    pallas_call x1, Pallas kernels, on_device(): pl.pallas_call(image_kernel, in_specs=[IN_VMEM, IN_VMEM], out_specs=pl.Bl...  2.27 us

profile of v1, /device:TPU:0, one launch (start us, length us, event | category | flops | bytes accessed | tf_op | source)
XLA Modules:
  0.0 44.9 jit_solution(12127212449734158434)
XLA Ops:
  0.0 3.4 %range_binning.1 = (f32[128,1024]{1,0:T(8,128)S(1)}, f32[8,1024]{1,0:T(8,128)S(1)}) custom-call(s32[1]{0:T(128)} %bitcast.base_ref, s32[64,128]{1,0:T(8,128)} %bitcast.6, s32[64,128]{1,0:T(8,128)} %bitcast.8, f32[1,8192]{1,0:T(1,128)} %bitcast.10, f32[2,8192]{1,0:T(2,128)} %refs_3_.2, s32[1,8192]{1,0:T(1,128)} %bitcast.7, s32[1,8192]{1,0:T(1,128)} %bitcast.9), custom_call_target="tpu_custom_call" | custom-call | tf_op jit(solution)/shard_map/range_binning/pallas_call | solution.py:304
  3.4 0.0 copy-start
  3.4 39.1 %core.1.x = f32[16,8,16,128]{3,2,1,0:T(8,128)S(1)} custom-call(f32[8,1024]{1,0:T(8,128)S(1)} %get-tuple-element.7.refs_0_, f32[128,1024]{1,0:T(8,128)S(1)} %get-tuple-element.8.refs_1_, s32[32,32]{1,0:T(8,128)} %refs_2_.1, s32[32,32]{1,0:T(8,128)} %refs_3_.3, f32[16,256,128]{2,1,0:T(8,128)} %refs_4_.1, bf16[2,4,256,128]{3,2,1,0:T(8,128)(2,1)} %constant.22.clone.refs_5_, ...), custom_call_target="tpu_custom_call" | custom-call | tf_op jit(solution)/shard_map/core/pallas_call | solution.py:802
  42.5 0.0 copy-done
  42.5 2.3 %image.1 = f32[2,512,256]{2,1,0:T(8,128)} custom-call(f32[16,8,16,128]{3,2,1,0:T(8,128)S(1)} %core.1.x, bf16[2,4,256,128]{3,2,1,0:T(8,128)(2,1)S(1)} %copy-done), custom_call_target="tpu_custom_call" | custom-call | tf_op jit(solution)/shard_map/image/pallas_call | solution.py:935
Async XLA Ops:
  3.4 39.1 %copy-start = (bf16[2,4,256,128]{3,2,1,0:T(8,128)(2,1)S(1)}, bf16[2,4,256,128]{3,2,1,0:T(8,128)(2,1)}, u32[]{:S(2)}) copy-start(bf16[2,4,256,128]{3,2,1,0:T(8,128)(2,1)} %constant.28.clone.table) | copy-start | bytes 1572868

commit v2 on v1

--- a/solution.py
+++ b/solution.py
@@ -171,22 +171,38 @@
     return hi, mid, rest - mid
 
 
+def turn(r, trig):
+    u = r * r
+    sn = r * horner(u, trig[0])
+    cs = horner(u, trig[1])
+    twice = sn + sn
+    return 1.0 - twice * sn, twice * cs
+
+
+def times(a, b):
+    return a[0] * b[0] - a[1] * b[1], a[0] * b[1] + a[1] * b[0]
+
+
 def echoes(data, base, bins, trig):
-    where, re_amp, im_amp, rel = (data[j : j + 1] for j in range(4))
-    re2, im2 = 2.0 * re_amp, 2.0 * im_amp
-    inverse = 0.5 / (rel + (base.astype(f32) + NEAR))
-    gain = inverse * -64.0
-    bend = inverse * (1.0 / 64.0)
     width = data.shape[1]
-    rows = lax.broadcasted_iota(jnp.int32, (bins, width), 0).astype(f32)
-    hot = jnp.where(rows == rel, 1.0, 0.0).astype(bf16)
-    hot = jnp.concatenate([hot, hot], 1)
-    for q in range(P_SIZE // 128):
-        parts = [[], []]
-        for p in range(0, 128, 16):
-            ids = lax.broadcasted_iota(jnp.int32, (16, width), 0)
-            along = (ids + (q * 128 + p - P_SIZE // 2)).astype(f32) * SPACING
-            offset = along - where
+    chunk = min(width, CHUNK // 4)
+    hots, tiles = [], [[[], []] for _ in range(P_SIZE // 128)]
+    for left in range(0, width, chunk):
+        where, re_amp, im_amp, rel = (data[j : j + 1, left : left + chunk] for j in range(4))
+        re2, im2 = 2.0 * re_amp, 2.0 * im_amp
+        inverse = 0.5 / (rel + (base.astype(f32) + NEAR))
+        gain = inverse * -64.0
+        gain2 = gain + gain
+        bend = inverse * (1.0 / 64.0)
+        rows = lax.broadcasted_iota(jnp.int32, (bins, chunk), 0).astype(f32)
+        hot = jnp.where(rows == rel, 1.0, 0.0).astype(bf16)
+        hots += [hot, hot]
+        odd = lax.broadcasted_iota(jnp.int32, (8, chunk), 0).astype(f32) * 2.0 + 1.0
+        even = turn(odd * odd * (SPACING * SPACING / 4.0) * gain, trig)
+        for q in range(P_SIZE // 128):
+            ids = lax.broadcasted_iota(jnp.int32, (16, chunk), 0)
+            middle = (ids * 8 + (q * 128 - P_SIZE // 2)).astype(f32) + 3.5
+            offset = middle * SPACING - where
             t = offset * offset * gain
             y = t * bend
             t = t * (1.0 + y * (1.0 + 2.0 * y))
@@ -194,13 +210,28 @@
             u = r * r
             sn = r * horner(u, trig[0])
             cs = horner(u, trig[1])
-            re = re_amp - sn * (re2 * sn + im2 * cs)
-            im = im_amp + sn * (re2 * cs - im2 * sn)
-            for c, v in enumerate((re, im)):
-                parts[c].append(jnp.concatenate(split(v), 1))
+            at = (re_amp - sn * (re2 * sn + im2 * cs), im_amp + sn * (re2 * cs - im2 * sn))
+            slope = offset * gain2 * (1.0 + y * (2.0 + 6.0 * y))
+            power = turn(slope * (SPACING / 2.0), trig)
+            square = (1.0 - 2.0 * power[1] * power[1], 2.0 * power[0] * power[1])
+            made = [None] * 8
+            for j in range(4):
+                a = times(at, (even[0][j : j + 1], even[1][j : j + 1]))
+                rr, ii = a[0] * power[0], a[1] * power[1]
+                ri, ir = a[0] * power[1], a[1] * power[0]
+                made[4 + j] = (rr - ii, ri + ir)
+                made[3 - j] = (rr + ii, ir - ri)
+                if j < 3:
+                    power = times(power, square)
+            for c in range(2):
+                tiles[q][c].append(
+                    jnp.concatenate([jnp.concatenate(split(v[c]), 1) for v in made], 0)
+                )
+    hot = jnp.concatenate(hots, 1)
+    for q in range(P_SIZE // 128):
         for c in range(2):
             lanes = slice(c * P_SIZE + q * 128, c * P_SIZE + (q + 1) * 128)
-            yield lanes, product(hot, jnp.concatenate(parts[c], 0), ((1,), (1,)))
+            yield lanes, product(hot, jnp.concatenate(tiles[q][c], 1), ((1,), (1,)))
 
 
 def range_bin_kernel(base_ref, *refs, span, trig):
@@ -457,8 +488,9 @@
     fwd, inv = [], []
     for low in range(4):
         a = 2 * np.pi / P_SIZE * (((4 * m[:, None] + low) * m[None, :]) % P_SIZE)
-        turn = a.reshape(-1, 2, q).transpose(1, 0, 2).reshape(q, q)
-        fwd.append(np.concatenate([np.cos(turn), np.sin(turn)], 0))
+        f = a.reshape(-1, 2, q).transpose(1, 0, 2).reshape(q, q // 8, 8)
+        f = f.transpose(0, 2, 1).reshape(q, q)
+        fwd.append(np.concatenate([np.cos(f), np.sin(f)], 0))
         inv.append(np.concatenate([np.cos(a.T), np.sin(a.T)], 0) / P_SIZE)
     return np.stack(fwd), np.stack(inv)
 

time: 45.2 us -> 43.5 us (0.962)
  Pallas kernels: 44.7 us -> 43.5 us
    pallas_call x1, Pallas kernels: 39.1 us -> 38.2 us  [core(): pl.pallas_call(functools.partial(core_kernel, n_pulse=n_pulse, n_scat=n_s...]
where the time goes in v2:
time: 43.5 us; the launch traced here: 43.6 us
  Pallas kernels  43.5 us (100%)
    pallas_call x1, Pallas kernels, core(): pl.pallas_call(functools.partial(core_kernel, n_pulse=n_pulse, n_scat=n_s...  38.2 us
    pallas_call x1, Pallas kernels, range_binning(): pl.pallas_call(functools.partial(range_bin_kernel, span=span, trig=range_...  3.03 us
    pallas_call x1, Pallas kernels, on_device(): pl.pallas_call(image_kernel, in_specs=[IN_VMEM, IN_VMEM], out_specs=pl.Bl...  2.28 us

profile of v2, /device:TPU:0, one launch (start us, length us, event | category | flops | bytes accessed | tf_op | source)
XLA Modules:
  0.0 43.6 jit_solution(8331807959429655479)
XLA Ops:
  0.0 3.0 %range_binning.1 = (f32[128,1024]{1,0:T(8,128)S(1)}, f32[8,1024]{1,0:T(8,128)S(1)}) custom-call(s32[1]{0:T(128)} %bitcast.base_ref, s32[64,128]{1,0:T(8,128)} %bitcast.6, s32[64,128]{1,0:T(8,128)} %bitcast.8, f32[1,8192]{1,0:T(1,128)} %bitcast.10, f32[2,8192]{1,0:T(2,128)} %refs_3_.2, s32[1,8192]{1,0:T(1,128)} %bitcast.7, s32[1,8192]{1,0:T(1,128)} %bitcast.9), custom_call_target="tpu_custom_call" | custom-call | tf_op jit(solution)/shard_map/range_binning/pallas_call | solution.py:335
  3.0 0.0 copy-start
  3.0 38.2 %core.1.x = f32[16,8,16,128]{3,2,1,0:T(8,128)S(1)} custom-call(f32[8,1024]{1,0:T(8,128)S(1)} %get-tuple-element.7.refs_0_, f32[128,1024]{1,0:T(8,128)S(1)} %get-tuple-element.8.refs_1_, s32[32,32]{1,0:T(8,128)} %refs_2_.1, s32[32,32]{1,0:T(8,128)} %refs_3_.3, f32[16,256,128]{2,1,0:T(8,128)} %refs_4_.1, bf16[2,4,256,128]{3,2,1,0:T(8,128)(2,1)} %constant.22.clone.refs_5_, ...), custom_call_target="tpu_custom_call" | custom-call | tf_op jit(solution)/shard_map/core/pallas_call | solution.py:834
  41.3 0.0 copy-done
  41.3 2.3 %image.1 = f32[2,512,256]{2,1,0:T(8,128)} custom-call(f32[16,8,16,128]{3,2,1,0:T(8,128)S(1)} %core.1.x, bf16[2,4,256,128]{3,2,1,0:T(8,128)(2,1)S(1)} %copy-done), custom_call_target="tpu_custom_call" | custom-call | tf_op jit(solution)/shard_map/image/pallas_call | solution.py:967
Async XLA Ops:
  3.0 38.2 %copy-start = (bf16[2,4,256,128]{3,2,1,0:T(8,128)(2,1)S(1)}, bf16[2,4,256,128]{3,2,1,0:T(8,128)(2,1)}, u32[]{:S(2)}) copy-start(bf16[2,4,256,128]{3,2,1,0:T(8,128)(2,1)} %constant.28.clone.table) | copy-start | bytes 1572868

commit v3 on v2

--- a/solution.py
+++ b/solution.py
@@ -18,8 +18,9 @@
 NEAR = 700000.0
 BIN_SIDE = 32
 GROUP = 4
-CHUNK = 1024
-SLOTS = 192
+CHUNK = 512
+SLOTS = 112
+LANES = 256
 WIDE = 128
 AHEAD = 1024
 SHARED = 1
@@ -185,7 +186,7 @@
 
 def echoes(data, base, bins, trig):
     width = data.shape[1]
-    chunk = min(width, CHUNK // 4)
+    chunk = min(width, LANES)
     hots, tiles = [], [[[], []] for _ in range(P_SIZE // 128)]
     for left in range(0, width, chunk):
         where, re_amp, im_amp, rel = (data[j : j + 1, left : left + chunk] for j in range(4))
@@ -248,7 +249,8 @@
         copy.wait()
     base = base_ref[0]
     rows = cells8.shape[0]
-    chunks = rows // 8
+    deep = CHUNK // 128
+    chunks = rows // deep
     target = cells8[...] + SHIFT * bounce8[...] - base
     match = jnp.where((target >= 0) & (target < span), 1.0, 0.0)
     mb = match.astype(bf16)
@@ -259,11 +261,11 @@
     total = jnp.dot(mb, jnp.ones((128, 128), bf16), preferred_element_type=f32)
     a = lax.broadcasted_iota(jnp.int32, (rows, rows), 0)
     b = lax.broadcasted_iota(jnp.int32, (rows, rows), 1)
-    below = jnp.where((a // 8 == b // 8) & (b < a), 1.0, 0.0).astype(bf16)
+    below = jnp.where((a // deep == b // deep) & (b < a), 1.0, 0.0).astype(bf16)
     ahead = jnp.dot(below, total.astype(bf16), preferred_element_type=f32)
     rank = jnp.where(match > 0.0, count + ahead - 1.0, -1.0)
     counts = [
-        jnp.sum(match[8 * c : 8 * c + 8]).astype(jnp.int32) for c in range(chunks)
+        jnp.sum(match[deep * c : deep * (c + 1)]).astype(jnp.int32) for c in range(chunks)
     ]
 
     def values(c):
@@ -279,7 +281,11 @@
     def pick(c, first):
         slots = lax.broadcasted_iota(jnp.int32, (SLOTS, 128), 0).astype(f32) + first
         hot = jnp.concatenate(
-            [jnp.where(rank[8 * c + j : 8 * c + j + 1] == slots, 1.0, 0.0) for j in range(8)], 1
+            [
+                jnp.where(rank[deep * c + j : deep * c + j + 1] == slots, 1.0, 0.0)
+                for j in range(deep)
+            ],
+            1,
         ).astype(bf16)
         return lax.dot_general(
             hot, values(c), (((1,), (1,)), ((), ())), preferred_element_type=f32
@@ -876,14 +882,15 @@
 
 
 def image_kernel(x, table, out, done, sems):
-    devs, kh, per, lanes = x.shape
+    lanes = x.shape[1]
+    per = x.shape[0] * GROUP // P_SIZE
     size = P_SIZE // 4
     copies = []
     for h in range(per // (2 * GROUP)):
         columns = [[] for _ in range(4)]
         for c in range(2):
             first = (2 * h + c) * GROUP
-            tiles = [x[:, :, first + j, :].reshape(devs * kh, lanes) for j in range(4)]
+            tiles = [x[pl.ds(first + j, size, stride=per), :] for j in range(4)]
             for k, z in enumerate(swap_blocks(tiles)):
                 columns[k].append(z)
         v = []
@@ -975,7 +982,7 @@
             ],
             compiler_params=pltpu.CompilerParams(vmem_limit_bytes=16 << 20),
             name="image",
-        )(columns, jnp.asarray(backward))
+        )(columns.reshape(-1, n), jnp.asarray(backward))
 
     ids = jnp.arange(GROUP, dtype=jnp.int32)[None, :, None] * BLOCKS
     first = stolt_block.reshape(groups, GROUP, BLOCKS) + ids

time: 43.5 us -> 43.1 us (level); the launches traced: 43.6 us -> 42.7 us
  Pallas kernels: 43.5 us -> 42.7 us
    pallas_call x1, Pallas kernels: 3.03 us -> 2.16 us  [range_binning(): pl.pallas_call(functools.partial(range_bin_kernel, span=span, trig=range_...]
where the time goes in v3:
time: 43.1 us; the launch traced here: 42.7 us
  Pallas kernels  42.7 us (99%)
    pallas_call x1, Pallas kernels, core(): pl.pallas_call(functools.partial(core_kernel, n_pulse=n_pulse, n_scat=n_s...  38.3 us
    pallas_call x1, Pallas kernels, on_device(): pl.pallas_call(image_kernel, in_specs=[IN_VMEM, IN_VMEM], out_specs=pl.Bl...  2.16 us
    pallas_call x1, Pallas kernels, range_binning(): pl.pallas_call(functools.partial(range_bin_kernel, span=span, trig=range_...  2.16 us

profile of v3, /device:TPU:0, one launch (start us, length us, event | category | flops | bytes accessed | tf_op | source)
XLA Modules:
  0.0 42.7 jit_solution(11881115174313757178)
XLA Ops:
  0.0 2.2 %range_binning.1 = (f32[128,1024]{1,0:T(8,128)S(1)}, f32[8,1024]{1,0:T(8,128)S(1)}) custom-call(s32[1]{0:T(128)} %bitcast.base_ref, s32[64,128]{1,0:T(8,128)} %bitcast.8, s32[64,128]{1,0:T(8,128)} %bitcast.10, f32[1,8192]{1,0:T(1,128)} %bitcast.12, f32[2,8192]{1,0:T(2,128)} %refs_3_.2, s32[1,8192]{1,0:T(1,128)} %bitcast.9, s32[1,8192]{1,0:T(1,128)} %bitcast.11), custom_call_target="tpu_custom_call" | custom-call | tf_op jit(solution)/shard_map/range_binning/pallas_call | solution.py:341
  2.2 0.0 copy-start
  2.2 38.3 %core.1 = f32[16,8,16,128]{3,2,1,0:T(8,128)S(1)} custom-call(f32[8,1024]{1,0:T(8,128)S(1)} %get-tuple-element.7.refs_0_, f32[128,1024]{1,0:T(8,128)S(1)} %get-tuple-element.8.refs_1_, s32[32,32]{1,0:T(8,128)} %refs_2_.1, s32[32,32]{1,0:T(8,128)} %refs_3_.3, f32[16,256,128]{2,1,0:T(8,128)} %refs_4_.1, bf16[2,4,256,128]{3,2,1,0:T(8,128)(2,1)} %constant.22.clone.refs_5_, ...), custom_call_target="tpu_custom_call" | custom-call | tf_op jit(solution)/shard_map/core/pallas_call | solution.py:840
  40.5 0.0 copy-done
  40.5 2.2 %image.1 = f32[2,512,256]{2,1,0:T(8,128)} custom-call(f32[2048,128]{1,0:T(8,128)S(1)} %bitcast.7, bf16[2,4,256,128]{3,2,1,0:T(8,128)(2,1)S(1)} %copy-done), custom_call_target="tpu_custom_call" | custom-call | tf_op jit(solution)/shard_map/image/pallas_call | solution.py:974
Async XLA Ops:
  2.2 38.4 %copy-start = (bf16[2,4,256,128]{3,2,1,0:T(8,128)(2,1)S(1)}, bf16[2,4,256,128]{3,2,1,0:T(8,128)(2,1)}, u32[]{:S(2)}) copy-start(bf16[2,4,256,128]{3,2,1,0:T(8,128)(2,1)} %constant.28.clone.table) | copy-start | bytes 1572868

commit v4 on v3

--- a/solution.py
+++ b/solution.py
@@ -20,9 +20,9 @@
 GROUP = 4
 CHUNK = 512
 SLOTS = 112
-LANES = 256
+LANES = 128
 WIDE = 128
-AHEAD = 1024
+AHEAD = 1152
 SHARED = 1
 STREAM = 512
 HIGH = lax.Precision.HIGH
@@ -524,10 +524,11 @@
     local = refs[13:23]
     steps_in, kinds_in, bank, table, ta, wa, tb, tc, wc, td = local
     binned, peer, spec, x, hot, kind, banks, os, twin_os, *twin_in = refs[23:34]
+    lone, twin_x = refs[34:36]
     (
         load, own_store, pair_send, pair_recv, near_send, near_recv, far_send, far_recv,
-        twin_send, twin_recv, half_send,
-    ) = refs[34:]
+        twin_send, twin_recv, half_send, lone_send,
+    ) = refs[36:]
     n_dev = n_pulse * n_scat
     pulse = lax.axis_index("pulse")
     scat = lax.axis_index("scat")
@@ -628,25 +629,32 @@
     def piece(dev, i):
         return pl.ds(pl.multiple_of((dev * pieces + i) * unit, unit), unit)
 
-    def source(p, c, i):
-        if i < pieces:
-            return piece(p * n_scat + c, i)
-        return piece(lax.rem(p + reach, n_pulse) * n_scat + c, pieces - 1)
+    for q in range(quads):
+        row = (pieces - 1) * unit + q * subs + subs - 1
+        lone[:, q, :] = spec[pl.ds(row, n_dev, stride=pieces * unit), :]
+
+    def twin_of(p, c):
+        return lax.rem(p + reach, n_pulse) * n_scat + c
 
     own = pl.ds(pl.multiple_of(me * unit, unit), unit)
     for i in range(pieces + 1):
         for j, (a, b) in enumerate(moves):
             p, c = other(a, b)
+            if i < pieces:
+                src, dst = spec.at[piece(p * n_scat + c, i), :], x.at[i, own, :]
+            else:
+                src, dst = lone.at[twin_of(p, c)], twin_x.at[me]
             pltpu.make_async_remote_copy(
-                src_ref=spec.at[source(p, c, i), :],
-                dst_ref=x.at[i, own, :],
-                send_sem=near_send.at[j],
+                src_ref=src,
+                dst_ref=dst,
+                send_sem=(near_send if i < pieces else lone_send).at[j],
                 recv_sem=near_recv.at[i, me],
                 device_id={"pulse": p, "scat": c},
                 device_id_type=MESH,
             ).start()
-    for i in range(pieces + 1):
-        x[i, own, :] = spec[source(pulse, scat, i), :]
+    for i in range(pieces):
+        x[i, own, :] = spec[piece(me, i), :]
+    twin_x[me] = lone[twin_of(pulse, scat)]
 
     for i in (2, 4, 5, 6, 7, 8, 9):
         loads[i].wait()
@@ -764,9 +772,13 @@
     served = pl.ds(pl.multiple_of(side * part, part), part)
 
     lax.fori_loop(0, groups - SHARED, step, 0)
-    if SHARED == subs:
-        arrived(pieces - 1)
-    arrived(pieces)
+    for a, b in moves:
+        p, c = other(a, b)
+        src = p * n_scat + c
+        pltpu.make_async_copy(
+            twin_x.at[src], twin_x.at[src], near_recv.at[pieces, src]
+        ).wait()
+    x[pieces, pl.ds(subs - 1, n_dev * quads, stride=subs), :] = twin_x[...].reshape(-1, n)
 
     def half_step(t, carry):
         v, h = lax.div(t, SHARED), lax.rem(t, SHARED)
@@ -808,8 +820,9 @@
     for j, (a, b) in enumerate(moves):
         p, c = other(a, b)
         src = p * n_scat + c
-        whole = spec.at[pl.ds(0, (pieces + 1) * unit), :]
+        whole = spec.at[pl.ds(0, pieces * unit), :]
         pltpu.make_async_copy(whole, whole, near_send.at[j]).wait()
+        pltpu.make_async_copy(lone.at[0], lone.at[0], lone_send.at[j]).wait()
         pltpu.make_async_copy(os.at[src], os.at[src], far_send.at[j]).wait()
         whole = out.at[src, first] if (a, b) == (reach, 0) else out.at[src]
         pltpu.make_async_copy(whole, whole, far_recv.at[src]).wait()
@@ -862,6 +875,8 @@
             pltpu.VMEM((2, n_dev // 2, SHARED, per, n), f32),
             pltpu.VMEM(steps_in.shape, steps_in.dtype),
             pltpu.VMEM(kinds_in.shape, kinds_in.dtype),
+            pltpu.VMEM((n_dev, quads, n), f32),
+            pltpu.VMEM((n_dev, quads, n), f32),
             dma((len(sources),)),
             dma((3,)),
             dma,
@@ -873,6 +888,7 @@
             dma((2,)),
             dma((2,)),
             dma((n_dev // 2,)),
+            dma((n_dev,)),
         ],
         compiler_params=pltpu.CompilerParams(
             collective_id=0, has_side_effects=True, vmem_limit_bytes=24 << 20

time: 43.1 us -> 42.4 us (0.984)
  Pallas kernels: 42.7 us -> 42.2 us
    pallas_call x1, Pallas kernels: 38.3 us -> 37.8 us  [core(): pl.pallas_call(functools.partial(core_kernel, n_pulse=n_pulse, n_scat=n_s...]
where the time goes in v4:
time: 42.4 us; the launch traced here: 42.2 us
  Pallas kernels  42.2 us (100%)
    pallas_call x1, Pallas kernels, core(): pl.pallas_call(functools.partial(core_kernel, n_pulse=n_pulse, n_scat=n_s...  37.8 us
    pallas_call x1, Pallas kernels, range_binning(): pl.pallas_call(functools.partial(range_bin_kernel, span=span, trig=range_...  2.2 us
    pallas_call x1, Pallas kernels, on_device(): pl.pallas_call(image_kernel, in_specs=[IN_VMEM, IN_VMEM], out_specs=pl.Bl...  2.19 us

profile of v4, /device:TPU:0, one launch (start us, length us, event | category | flops | bytes accessed | tf_op | source)
XLA Modules:
  0.0 42.2 jit_solution(6909703446993339135)
XLA Ops:
  0.0 2.2 %range_binning.1 = (f32[128,1024]{1,0:T(8,128)S(1)}, f32[8,1152]{1,0:T(8,128)S(1)}) custom-call(s32[1]{0:T(128)} %bitcast.base_ref, s32[64,128]{1,0:T(8,128)} %bitcast.8, s32[64,128]{1,0:T(8,128)} %bitcast.10, f32[1,8192]{1,0:T(1,128)} %bitcast.12, f32[2,8192]{1,0:T(2,128)} %refs_3_.2, s32[1,8192]{1,0:T(1,128)} %bitcast.9, s32[1,8192]{1,0:T(1,128)} %bitcast.11), custom_call_target="tpu_custom_call" | custom-call | tf_op jit(solution)/shard_map/range_binning/pallas_call | solution.py:341
  2.2 0.0 copy-start
  2.2 37.8 %core.1 = f32[16,8,16,128]{3,2,1,0:T(8,128)S(1)} custom-call(f32[8,1152]{1,0:T(8,128)S(1)} %get-tuple-element.7.refs_0_, f32[128,1024]{1,0:T(8,128)S(1)} %get-tuple-element.8.refs_1_, s32[32,32]{1,0:T(8,128)} %refs_2_.1, s32[32,32]{1,0:T(8,128)} %refs_3_.3, f32[16,256,128]{2,1,0:T(8,128)} %refs_4_.1, bf16[2,4,256,128]{3,2,1,0:T(8,128)(2,1)} %constant.22.clone.refs_5_, ...), custom_call_target="tpu_custom_call" | custom-call | tf_op jit(solution)/shard_map/core/pallas_call | solution.py:853
  40.0 0.0 copy-done
  40.1 2.2 %image.1 = f32[2,512,256]{2,1,0:T(8,128)} custom-call(f32[2048,128]{1,0:T(8,128)S(1)} %bitcast.7, bf16[2,4,256,128]{3,2,1,0:T(8,128)(2,1)S(1)} %copy-done), custom_call_target="tpu_custom_call" | custom-call | tf_op jit(solution)/shard_map/image/pallas_call | solution.py:990
Async XLA Ops:
  2.2 37.8 %copy-start = (bf16[2,4,256,128]{3,2,1,0:T(8,128)(2,1)S(1)}, bf16[2,4,256,128]{3,2,1,0:T(8,128)(2,1)}, u32[]{:S(2)}) copy-start(bf16[2,4,256,128]{3,2,1,0:T(8,128)(2,1)} %constant.28.clone.table) | copy-start | bytes 1572868

commit v5 on v4

--- a/solution.py
+++ b/solution.py
@@ -502,19 +502,21 @@
 
 
 def swap_blocks(arrays):
+    arrays = list(arrays)
     count = len(arrays)
     lanes = arrays[0].shape[-1]
-    size = lanes // count
-    block = lax.broadcasted_iota(jnp.int32, arrays[0].shape, 1) // size
-    outs = []
-    for b in range(count):
-        acc = None
-        for a in range(count):
-            shift = (a - b) % count * size
-            moved = pltpu.roll(arrays[a], shift, 1) if shift else arrays[a]
-            acc = moved if acc is None else jnp.where(block == a, moved, acc)
-        outs.append(acc)
-    return outs
+    block = lax.broadcasted_iota(jnp.int32, arrays[0].shape, 1) // (lanes // count)
+    step = count // 2
+    while step:
+        shift = step * (lanes // count)
+        low = block // step % 2 == 0
+        for i in range(count):
+            if i // step % 2 == 0:
+                a, b = arrays[i], arrays[i + step]
+                arrays[i] = jnp.where(low, a, pltpu.roll(b, shift, 1))
+                arrays[i + step] = jnp.where(low, pltpu.roll(a, lanes - shift, 1), b)
+        step //= 2
+    return arrays
 
 
 def core_kernel(*refs, n_pulse, n_scat, subs, trig, trig_low):

time: 42.4 us -> 42.1 us (level)
  no operation moved by 1% of the time
where the time goes in v5:
time: 42.1 us; the launch traced here: 42 us
  Pallas kernels  41.9 us (100%)
    pallas_call x1, Pallas kernels, core(): pl.pallas_call(functools.partial(core_kernel, n_pulse=n_pulse, n_scat=n_s...  37.8 us
    pallas_call x1, Pallas kernels, range_binning(): pl.pallas_call(functools.partial(range_bin_kernel, span=span, trig=range_...  2.2 us
    pallas_call x1, Pallas kernels, on_device(): pl.pallas_call(image_kernel, in_specs=[IN_VMEM, IN_VMEM], out_specs=pl.Bl...  1.91 us

profile of v5, /device:TPU:0, one launch (start us, length us, event | category | flops | bytes accessed | tf_op | source)
XLA Modules:
  0.0 42.0 jit_solution(3564388722618283652)
XLA Ops:
  0.0 2.2 %range_binning.1 = (f32[128,1024]{1,0:T(8,128)S(1)}, f32[8,1152]{1,0:T(8,128)S(1)}) custom-call(s32[1]{0:T(128)} %bitcast.base_ref, s32[64,128]{1,0:T(8,128)} %bitcast.8, s32[64,128]{1,0:T(8,128)} %bitcast.10, f32[1,8192]{1,0:T(1,128)} %bitcast.12, f32[2,8192]{1,0:T(2,128)} %refs_3_.2, s32[1,8192]{1,0:T(1,128)} %bitcast.9, s32[1,8192]{1,0:T(1,128)} %bitcast.11), custom_call_target="tpu_custom_call" | custom-call | tf_op jit(solution)/shard_map/range_binning/pallas_call | solution.py:341
  2.2 0.0 copy-start
  2.2 37.8 %core.1 = f32[16,8,16,128]{3,2,1,0:T(8,128)S(1)} custom-call(f32[8,1152]{1,0:T(8,128)S(1)} %get-tuple-element.7.refs_0_, f32[128,1024]{1,0:T(8,128)S(1)} %get-tuple-element.8.refs_1_, s32[32,32]{1,0:T(8,128)} %refs_2_.1, s32[32,32]{1,0:T(8,128)} %refs_3_.3, f32[16,256,128]{2,1,0:T(8,128)} %refs_4_.1, bf16[2,4,256,128]{3,2,1,0:T(8,128)(2,1)} %constant.22.clone.refs_5_, ...), custom_call_target="tpu_custom_call" | custom-call | tf_op jit(solution)/shard_map/core/pallas_call | solution.py:855
  40.1 0.0 copy-done
  40.1 1.9 %image.1 = f32[2,512,256]{2,1,0:T(8,128)} custom-call(f32[2048,128]{1,0:T(8,128)S(1)} %bitcast.7, bf16[2,4,256,128]{3,2,1,0:T(8,128)(2,1)S(1)} %copy-done), custom_call_target="tpu_custom_call" | custom-call | tf_op jit(solution)/shard_map/image/pallas_call | solution.py:992
Async XLA Ops:
  2.2 37.9 %copy-start = (bf16[2,4,256,128]{3,2,1,0:T(8,128)(2,1)S(1)}, bf16[2,4,256,128]{3,2,1,0:T(8,128)(2,1)}, u32[]{:S(2)}) copy-start(bf16[2,4,256,128]{3,2,1,0:T(8,128)(2,1)} %constant.28.clone.table) | copy-start | bytes 1572868
